TPU v7x, 512 devices: a whole 4x4x16 slice. The times are simulated.
512 devices in a mesh: seqa: 16 (over z_lo, core), seqb: 8 (over x, z_hi), dp: 4 (over y).
Axes of the slice: x: 4, y: 4, z: 16 (z_hi: 2, z_lo: 8; z = z_hi * 8 + z_lo), core: 2. Of those that a mesh axis runs over, the one named last changes fastest.
Arguments:
- queries: bfloat16 [16384, 128, 64], P(('dp', 'seqa', 'seqb')), parts along dimension 0, may hold values from -6 to 6
- keys: bfloat16 [16384, 128, 64], P(('dp', 'seqa', 'seqb')), parts along dimension 0, may hold values from -6 to 6
- values: bfloat16 [16384, 128, 64], P(('dp', 'seqa', 'seqb')), parts along dimension 0, may hold values from -6 to 6
- doc_bounds: int32 [36], P('dp'), parts along dimension 0, may hold values from 0 to 4096, as said below
- q_gain: float32 [64], replicated, may hold values from 0.25 to 1.75
- k_gain: float32 [64], replicated, may hold values from 0.25 to 1.75
Outputs:
- attended: bfloat16 [16384, 128, 64], P(('dp', 'seqa', 'seqb')), parts along dimension 0
There are 4 independent parts, one for each index of `dp`. A program takes and returns all parts, laid end to end along the dimension named above; an argument that names none is the same for every part. Nothing has to cross between parts.
Inputs may be any that keep to these rules, and one draw needn't show every extreme that they name: doc_bounds[0] is 0, doc_bounds[8] is 4096, and the entries rise strictly.
All inputs are finite; a program needn't handle non-finite values.
Results may differ from a plain program's by a relative error of at most 0.0015.
Values may be sent and summed in bfloat16 or wider, within the bound.
A program may use at most 64 MiB of HBM per device.

v0:
```python
import functools

import jax
import jax.numpy as jnp
from jax import lax
from jax.experimental import pallas as pl
from jax.experimental.pallas import tpu as pltpu
from jax.sharding import PartitionSpec as P

MESH = pl.DeviceIdType.MESH
TOK_DEV = 32
DOCS = 8


def cos_sin(angle):
    turns = jnp.floor(angle * 0.6366197723675814 + 0.5)
    r = angle - turns * 1.5703125
    r = r - turns * 4.837512969970703125e-4
    r = r - turns * 7.54978995489188216e-8
    z = r * r
    s = ((-1.9515295891e-4 * z + 8.3321608736e-3) * z - 1.6666654611e-1) * z * r + r
    c = ((2.443315711809948e-5 * z - 1.388731625493765e-3) * z + 4.166664568298827e-2) * z * z
    c = c - 0.5 * z + 1.0
    quarter = turns.astype(jnp.int32)
    odd = (quarter & 1) == 1
    cosine = jnp.where(odd, s, c)
    sine = jnp.where(odd, c, s)
    cosine = jnp.where(((quarter + 1) & 2) == 2, -cosine, cosine)
    sine = jnp.where((quarter & 2) == 2, -sine, sine)
    return cosine, sine


def starts_of(places, doc):
    start = jnp.zeros_like(places)
    for d in range(1, doc.shape[0] - 1):
        start = jnp.where(places >= doc[d], doc[d], start)
    return start


def kernel(
    nb, q_hbm, k_hbm, v_hbm, doc_hbm, qg_hbm, kg_hbm, out_ref,
    qb, kb, vb, doc, qg, kg, rows_qk, rows_v, send, recv, back, gathered, rows_out,
    in_sem, send_sem, recv_sem, back_send, back_recv,
):
    tok, heads, width = qb.shape
    n = recv.shape[0]
    half, pair = tok // 2, 2 * width
    me = lax.axis_index("seqa") * nb + lax.axis_index("seqb")

    def place(m):
        peer = lax.rem(me + m, n)
        return peer, {"seqa": peer // nb, "seqb": lax.rem(peer, nb)}

    barrier = pltpu.get_barrier_semaphore()
    for m in range(1, n):
        pl.semaphore_signal(barrier, inc=1, device_id=place(m)[1], device_id_type=MESH)
    loads = [
        pltpu.make_async_copy(src, dst, in_sem.at[i])
        for i, (src, dst) in enumerate(
            ((doc_hbm, doc), (qg_hbm, qg), (kg_hbm, kg), (q_hbm, qb), (k_hbm, kb), (v_hbm, vb))
        )
    ]
    for load in loads:
        load.start()
    for load in loads[:3]:
        load.wait()

    lane = lax.broadcasted_iota(jnp.int32, (tok, pair), 1)
    low = lane < width
    places = me * tok + lax.broadcasted_iota(jnp.int32, (tok, pair), 0)
    within = lax.rem(lane, width // 2).astype(jnp.float32)
    freq = jnp.exp(within * (-2.0 / width * 9.210340371976184))
    cosine, sine = cos_sin((places - starts_of(places, doc)).astype(jnp.float32) * freq)
    first = lax.rem(lane, width) < width // 2
    sine = jnp.where(first, -sine, sine)
    gain = jnp.concatenate([qg[...] * width**-0.5, kg[...]], axis=-1)

    for load in loads[3:]:
        load.wait()
    rows_qk[:, :width] = qb[...].astype(jnp.float32).reshape(tok * heads, width)
    rows_qk[:, width:] = kb[...].astype(jnp.float32).reshape(tok * heads, width)
    rows_v[...] = vb[...].astype(jnp.float32).reshape(tok * heads, width)
    for h in range(heads):
        x = rows_qk[pl.ds(h, tok, stride=heads), :]
        v = rows_v[pl.ds(h, tok, stride=heads), :]
        square = x * x
        total_q = jnp.sum(jnp.where(low, square, 0.0), axis=-1, keepdims=True)
        total_k = jnp.sum(jnp.where(low, 0.0, square), axis=-1, keepdims=True)
        x = x * lax.rsqrt(jnp.where(low, total_q, total_k) / width + 1e-06) * gain
        other = jnp.where(
            first, pltpu.roll(x, pair - width // 2, 1), pltpu.roll(x, width // 2, 1)
        )
        x = x * cosine + other * sine
        kv = jnp.concatenate([x[:, width:], v], axis=-1)
        qq = jnp.concatenate([x[:half, :width], x[half:, :width]], axis=-1)
        send[h, :tok, :] = kv.astype(jnp.bfloat16)
        send[h, tok:, :] = qq.astype(jnp.bfloat16)
    recv[me] = send[me]

    q_places = [
        lax.broadcasted_iota(jnp.int32, (n, half, 1), 0) * tok
        + lax.broadcasted_iota(jnp.int32, (n, half, 1), 1)
        + part * half
        for part in range(2)
    ]
    q_places = [x.reshape(n * half, 1) for x in q_places]
    q_starts = [starts_of(x, doc) for x in q_places]

    pl.semaphore_wait(barrier, n - 1)

    def exchange(source, target, sems, m):
        peer, coords = place(m)
        return pltpu.make_async_remote_copy(
            src_ref=source.at[peer],
            dst_ref=target.at[me],
            send_sem=sems[0].at[m - 1],
            recv_sem=sems[1].at[m - 1],
            device_id=coords,
            device_id_type=MESH,
        )

    out = [exchange(send, recv, (send_sem, recv_sem), m) for m in range(1, n)]
    for copy in out:
        copy.start()
    for copy in out:
        copy.wait_recv()

    outs = []
    for part in range(2):
        kv = recv[:, :tok, :].reshape(n * tok, pair)
        q = recv[:, tok:, part * width : (part + 1) * width].reshape(n * half, width)
        scores = lax.dot_general(
            q, kv[:, :width], (((1,), (1,)), ((), ())), preferred_element_type=jnp.float32
        )
        key = lax.broadcasted_iota(jnp.int32, scores.shape, 1)
        allowed = (key >= q_starts[part]) & (key <= q_places[part])
        expo = jnp.where(allowed, jnp.exp(scores), 0.0)
        weights = (expo * (1.0 / jnp.sum(expo, axis=1, keepdims=True))).astype(jnp.bfloat16)
        both = jnp.dot(weights, kv, preferred_element_type=jnp.float32)
        outs.append(both[:, width:])
    back[...] = (
        jnp.concatenate(outs, axis=-1).astype(jnp.bfloat16).reshape(n, half, pair)
    )
    home = [exchange(back, gathered, (back_send, back_recv), m) for m in range(1, n)]
    for copy in home:
        copy.start()
    gathered[me] = back[me]
    for copy in out:
        copy.wait_send()
    for copy in home:
        copy.wait_recv()
    for h in range(heads):
        block = gathered[h].astype(jnp.float32)
        rows_out[pl.ds(h, half, stride=heads), :] = block[:, :width]
        rows_out[pl.ds(half * heads + h, half, stride=heads), :] = block[:, width:]
    out_ref[...] = rows_out[...].reshape(tok, heads, width).astype(jnp.bfloat16)
    for copy in home:
        copy.wait_send()


def fused(n, nb, queries, keys, values, doc_bounds, q_gain, k_gain):
    tok, heads, width = queries.shape
    half, pair = tok // 2, 2 * width
    block = pltpu.VMEM((tok, heads, width), jnp.bfloat16)
    dma = pltpu.SemaphoreType.DMA((n - 1,))
    return pl.pallas_call(
        functools.partial(kernel, nb),
        out_shape=jax.ShapeDtypeStruct(queries.shape, queries.dtype),
        in_specs=[pl.BlockSpec(memory_space=pl.ANY)] * 6,
        out_specs=pl.BlockSpec(memory_space=pltpu.VMEM),
        scratch_shapes=[
            block, block, block,
            pltpu.SMEM(doc_bounds.shape, jnp.int32),
            pltpu.VMEM((1, width), jnp.float32),
            pltpu.VMEM((1, width), jnp.float32),
            pltpu.VMEM((tok * heads, pair), jnp.float32),
            pltpu.VMEM((tok * heads, width), jnp.float32),
            pltpu.VMEM((n, tok + half, pair), jnp.bfloat16),
            pltpu.VMEM((n, tok + half, pair), jnp.bfloat16),
            pltpu.VMEM((n, half, pair), jnp.bfloat16),
            pltpu.VMEM((n, half, pair), jnp.bfloat16),
            pltpu.VMEM((tok * heads, width), jnp.float32),
            pltpu.SemaphoreType.DMA((6,)),
            dma, dma, dma, dma,
        ],
        compiler_params=pltpu.CompilerParams(collective_id=0, has_side_effects=True),
    )(queries, keys, values, doc_bounds, q_gain.reshape(1, width), k_gain.reshape(1, width))


def for_sending(value):
    return jax.tree.map(lambda a: a.astype(jnp.bfloat16) if a.dtype == jnp.float32 else a, value)


def prepare(block, gain, positions):
    values32 = block.astype(jnp.float32)
    scale = lax.rsqrt(jnp.mean(values32 * values32, axis=-1, keepdims=True) + 1e-06)
    normed = values32 * scale * gain
    half = normed.shape[-1] // 2
    freq = jnp.exp(-jnp.log(10000.0) * jnp.arange(half, dtype=jnp.float32) * 2.0 / normed.shape[-1])
    angle = positions.astype(jnp.float32)[:, None] * freq[None, :]
    first = normed[:, :half]
    second = normed[:, half:]
    cosine = jnp.cos(angle)
    sine = jnp.sin(angle)
    rotated = jnp.concatenate(
        [first * cosine - second * sine, first * sine + second * cosine], axis=-1
    )
    return rotated.astype(jnp.bfloat16)


def attend_head(query_head, key_head, value_head, doc_bounds, q_gain, k_gain):
    length, width = query_head.shape
    places = jnp.arange(length, dtype=jnp.int32)
    doc = jnp.sum((places[:, None] >= doc_bounds[None, 1:DOCS]).astype(jnp.int32), axis=1).astype(
        jnp.int32
    )
    positions = places - doc_bounds[doc]
    qr = prepare(query_head, q_gain, positions)
    kr = prepare(key_head, k_gain, positions)
    block = 8 * TOK_DEV
    count = length // block

    def one_block(items):
        query_rows, query_doc, query_place = items
        scores = jnp.dot(query_rows, kr.T, preferred_element_type=jnp.float32) / jnp.sqrt(
            jnp.float32(width)
        )
        allowed = (query_doc[:, None] == doc[None, :]) & (places[None, :] <= query_place[:, None])
        scores = jnp.where(allowed, scores, jnp.float32(-1e30))
        top = jnp.max(scores, axis=1, keepdims=True)
        expo = jnp.where(allowed, jnp.exp(scores - top), jnp.float32(0.0))
        weights = (expo / jnp.sum(expo, axis=1, keepdims=True)).astype(jnp.bfloat16)
        return jnp.dot(weights, value_head, preferred_element_type=jnp.float32).astype(jnp.bfloat16)

    outputs = lax.map(
        one_block,
        (qr.reshape(count, block, width), doc.reshape(count, block), places.reshape(count, block)),
    )
    return outputs.reshape(length, width)


def body(queries, keys, values, doc_bounds, q_gain, k_gain):
    query_full, key_full, value_full = (
        lax.all_to_all(queries, ("seqa", "seqb"), split_axis=1, concat_axis=0, tiled=True),
        lax.all_to_all(keys, ("seqa", "seqb"), split_axis=1, concat_axis=0, tiled=True),
        lax.all_to_all(values, ("seqa", "seqb"), split_axis=1, concat_axis=0, tiled=True),
    )
    attend_all = jax.vmap(attend_head, in_axes=(1, 1, 1, None, None, None), out_axes=1)
    result = attend_all(query_full, key_full, value_full, doc_bounds, q_gain, k_gain)
    back = jax.tree.map(
        lambda part, own: part.astype(own.dtype),
        lax.all_to_all(
            for_sending(result), ("seqa", "seqb"), split_axis=0, concat_axis=1, tiled=True
        ),
        result,
    )
    return back


def solution(mesh):
    placed = (
        P(("dp", "seqa", "seqb"), None, None),
        P(("dp", "seqa", "seqb"), None, None),
        P(("dp", "seqa", "seqb"), None, None),
        P("dp"),
        P(),
        P(),
    )
    nb = mesh.shape["seqb"]
    n = mesh.shape["seqa"] * nb

    def local(queries, keys, values, doc_bounds, q_gain, k_gain):
        tok, heads, width = queries.shape
        fits = heads == n and heads == 8 and tok % 32 == 0 and n * tok <= 512 and width == 64
        step = functools.partial(fused, n, nb) if fits else body
        return step(queries, keys, values, doc_bounds, q_gain, k_gain)

    return jax.shard_map(
        local,
        mesh=mesh,
        in_specs=placed,
        out_specs=P(("dp", "seqa", "seqb"), None, None),
        check_vma=False,
    )
```

profile of v0, /device:TPU:1, one launch (start us, length us, event | category | flops | bytes accessed | tf_op | source)
XLA Modules:
  0.0 308.2 jit_solution(3583680308432293283)
XLA Ops:
  0.0 2.5 copy.59
  3.9 20.4 %all-to-all-start = ((bf16[128,2,1024]{2,1,0:T(2,128)(2,1)}), bf16[128,2,1024]{2,1,0:T(2,128)(2,1)S(1)}, u32[]{:S(2)}, u32[]{:S(2)}) async-start(bf16[128,2,1024]{2,1,0:T(2,128)(2,1)} %reshape.490), calls=%async_computation | async-start | bytes 1048576 | tf_op jit(solution)/shard_map/all_to_all | solution.py:244
  27.5 31.3 %all-to-all-done = bf16[128,2,1024]{2,1,0:T(2,128)(2,1)S(1)} async-done(((bf16[128,2,1024]{2,1,0:T(2,128)(2,1)}), bf16[128,2,1024]{2,1,0:T(2,128)(2,1)S(1)}, u32[]{:S(2)}, u32[]{:S(2)}) %all-to-all-start) | async-done | bytes 524320 | tf_op jit(solution)/shard_map/all_to_all | solution.py:244
  58.8 6.4 %all-to-all-start.1 = ((bf16[128,2,1024]{2,1,0:T(2,128)(2,1)}), bf16[128,2,1024]{2,1,0:T(2,128)(2,1)}, u32[]{:S(2)}, u32[]{:S(2)}) async-start(bf16[128,2,1024]{2,1,0:T(2,128)(2,1)} %reshape.492), calls=%async_computation.1 | async-start | bytes 1048576 | tf_op jit(solution)/shard_map/all_to_all | solution.py:245
  69.1 4.6 %compare_select_fusion.1 = (s32[4096,1]{0,1:T(1,128)S(1)}, s32[4096,1]{0,1:T(1,128)S(1)}) fusion(s32[]{:T(128)} %bitcast.7, s32[]{:T(128)} %bitcast.8, s32[]{:T(128)} %bitcast.9, s32[]{:T(128)} %bitcast.10, s32[]{:T(128)} %bitcast.11, s32[]{:T(128)} %bitcast.13, s32[]{:T(128)} %bitcast.12, s32[4096,1]{0,1:T(1,128)S(1)} %bitcast.90), kind=kLoop, calls=%fused_computation.49 | loop fusion | flops 61440 | bytes 49180 | tf_op jit(solution)/shard_map/vmap()/gather | solution.py:217
  76.7 20.9 %all-to-all-done.1 = bf16[128,2,1024]{2,1,0:T(2,128)(2,1)} async-done(((bf16[128,2,1024]{2,1,0:T(2,128)(2,1)}), bf16[128,2,1024]{2,1,0:T(2,128)(2,1)}, u32[]{:S(2)}, u32[]{:S(2)}) %all-to-all-start.1) | async-done | bytes 524320 | tf_op jit(solution)/shard_map/all_to_all | solution.py:245
  97.5 6.6 %all-to-all-start.2 = ((bf16[128,2,1024]{2,1,0:T(2,128)(2,1)}), bf16[128,2,1024]{2,1,0:T(2,128)(2,1)}, u32[]{:S(2)}, u32[]{:S(2)}) async-start(bf16[128,2,1024]{2,1,0:T(2,128)(2,1)} %reshape.494), calls=%async_computation.2 | async-start | bytes 1048576 | tf_op jit(solution)/shard_map/all_to_all | solution.py:246
  104.2 2.3 reshape.493
  109.3 2.2 copy.68
  112.4 2.4 fusion.28
  117.7 19.6 %all-to-all-done.2 = bf16[128,2,1024]{2,1,0:T(2,128)(2,1)} async-done(((bf16[128,2,1024]{2,1,0:T(2,128)(2,1)}), bf16[128,2,1024]{2,1,0:T(2,128)(2,1)}, u32[]{:S(2)}, u32[]{:S(2)}) %all-to-all-start.2) | async-done | bytes 524320 | tf_op jit(solution)/shard_map/all_to_all | solution.py:246
  137.4 2.3 reshape.495
  139.6 99.7 %while.11 = (s32[]{:T(128)}, bf16[16,1,256,64]{2,3,1,0:T(8,128)(2,1)}, s32[16,256]{1,0:T(8,128)S(1)}, s32[4096]{0:T(1024)S(1)}, s32[16,256]{1,0:T(8,128)S(1)}, /...) while((s32[]{:T(128)}, ...), condition=%wide.region_6.7_spmd.clone, body=%wide.region_3.6_spmd.clone.sunk | while | flops 288374272 | bytes 13794917 | solution.py:235
  139.6 2.5 fusion.39
  143.6 2.3 fusion.41
  145.9 2.5 fusion.39
  149.8 2.3 fusion.41
  152.1 2.5 fusion.39
  156.0 2.3 fusion.41
  158.3 2.5 fusion.39
  162.2 2.3 fusion.41
  164.6 2.5 fusion.39
  168.5 2.3 fusion.41
  170.8 2.5 fusion.39
  174.7 2.3 fusion.41
  177.0 2.5 fusion.39
  180.9 2.3 fusion.41
  183.3 2.5 fusion.39
  187.2 2.3 fusion.41
  189.5 2.5 fusion.39
  193.4 2.3 fusion.41
  195.7 2.5 fusion.39
  199.6 2.3 fusion.41
  202.0 2.5 fusion.39
  205.9 2.3 fusion.41
  208.2 2.5 fusion.39
  212.1 2.3 fusion.41
  214.4 2.5 fusion.39
  218.3 2.3 fusion.41
  220.7 2.5 fusion.39
  224.6 2.3 fusion.41
  226.9 2.5 fusion.39
  230.8 2.3 fusion.41
  233.1 2.5 fusion.39
  237.0 2.3 fusion.41
  241.9 22.6 %reduce.16 = bf16[4096,64]{1,0:T(8,128)(2,1)S(1)} reduce(bf16[4096,1,64]{2,1,0:T(2,128)(2,1)S(1)} %reshape.484, bf16[]{:T(256)} %broadcast.313), dimensions={1}, to_apply=%reshape.484.reduce_sub_computation | reduce | bytes 1048578 | tf_op jit(solution)/shard_map/vmap()/transpose;vmap()/reshape;vmap()/transpose | solution.py:249
  265.1 39.9 %all_to_all.51 = bf16[128,2,1024]{2,1,0:T(2,128)(2,1)S(1)} all-to-all(bf16[128,2,1024]{2,1,0:T(2,128)(2,1)S(1)} %reshape.496), channel_id=1, replica_groups=mesh['seqa'=16,'seqb'=8,'dp'=4] {'seqa','seqb'}, dimensions={0} | all-to-all | bytes 1048576 | tf_op jit(solution)/shard_map/all_to_all | solution.py:252
  306.4 1.9 copy.73
  (82 shorter events, 44.5 us)
Async XLA Ops:
  0.0 24.3 %copy-start.2 = (s32[9]{0:T(128)S(1)}, s32[9]{0:T(128)}, u32[]{:S(2)}) copy-start(s32[9]{0:T(128)} %param.11) | copy-start | bytes 112
  0.0 24.4 %copy-start = (bf16[32,128,64]{1,2,0:T(8,128)(2,1)S(1)}, bf16[32,128,64]{1,2,0:T(8,128)(2,1)}, u32[]{:S(2)}) copy-start(bf16[32,128,64]{1,2,0:T(8,128)(2,1)} %param.9) | copy-start | bytes 1572868
  0.0 65.4 %copy-start.1 = (bf16[32,128,64]{1,2,0:T(8,128)(2,1)S(1)}, bf16[32,128,64]{1,2,0:T(8,128)(2,1)}, u32[]{:S(2)}) copy-start(bf16[32,128,64]{1,2,0:T(8,128)(2,1)} %param.10) | copy-start | bytes 1572868
  3.9 54.9 %all-to-all-start = ((bf16[128,2,1024]{2,1,0:T(2,128)(2,1)}), bf16[128,2,1024]{2,1,0:T(2,128)(2,1)S(1)}, u32[]{:S(2)}, u32[]{:S(2)}) async-start(bf16[128,2,1024]{2,1,0:T(2,128)(2,1)} %reshape.490), calls=%async_computation | async-start | bytes 1048576 | tf_op jit(solution)/shard_map/all_to_all | solution.py:244
  58.8 38.7 %all-to-all-start.1 = ((bf16[128,2,1024]{2,1,0:T(2,128)(2,1)}), bf16[128,2,1024]{2,1,0:T(2,128)(2,1)}, u32[]{:S(2)}, u32[]{:S(2)}) async-start(bf16[128,2,1024]{2,1,0:T(2,128)(2,1)} %reshape.492), calls=%async_computation.1 | async-start | bytes 1048576 | tf_op jit(solution)/shard_map/all_to_all | solution.py:245
  97.5 39.8 %all-to-all-start.2 = ((bf16[128,2,1024]{2,1,0:T(2,128)(2,1)}), bf16[128,2,1024]{2,1,0:T(2,128)(2,1)}, u32[]{:S(2)}, u32[]{:S(2)}) async-start(bf16[128,2,1024]{2,1,0:T(2,128)(2,1)} %reshape.494), calls=%async_computation.2 | async-start | bytes 1048576 | tf_op jit(solution)/shard_map/all_to_all | solution.py:246
  108.1 3.9 %copy-start.3 = (f32[64]{0:T(128)S(1)}, f32[64]{0:T(128)}, u32[]{:S(2)}) copy-start(f32[64]{0:T(128)} %param.13) | copy-start | bytes 772
  108.1 4.0 %copy-start.4 = (f32[64]{0:T(128)S(1)}, f32[64]{0:T(128)}, u32[]{:S(2)}) copy-start(f32[64]{0:T(128)} %param.12) | copy-start | bytes 772
where the time goes:
time: 309 us; the launch traced here: 308 us
  matrix products  77.5 us (25%)
  waiting for transfers between devices  71.8 us (23%)
  other arithmetic  57.5 us (19%)
  blocking collectives  39.9 us (13%)
  starting transfers between devices  33.4 us (11%)
  local copies, waits for them, and re-layouts  27.8 us (9%)
    dot_general x16, matrix products, one_block(): jnp.dot(query_rows, kr.T, preferred_element_type=jnp.float32)  40.5 us
    all_to_all x1, blocking collectives, body(): lax.all_to_all(for_sending(result), ('seqa', 'seqb'), split_axis=0, conca...  39.9 us
    dot_general x16, matrix products, one_block(): jnp.dot(weights, value_head, preferred_element_type=jnp.float32)  37 us
    all_to_all x1, waiting for transfers between devices, body(): lax.all_to_all(queries, ('seqa', 'seqb'), split_axis=1, concat_axis=0, ti...  31.3 us
    transpose x1, other arithmetic, body(): attend_all(query_full, key_full, value_full, doc_bounds, q_gain, k_gain)  22.6 us
    reduce_sum x16, other arithmetic, one_block(): weights = (expo / jnp.sum(expo, axis=1, keepdims=True)).astype(jnp.bfloat16)  22.1 us
    all_to_all x1, waiting for transfers between devices, body(): lax.all_to_all(keys, ('seqa', 'seqb'), split_axis=1, concat_axis=0, tiled...  20.9 us
    all_to_all x1, starting transfers between devices, body(): lax.all_to_all(queries, ('seqa', 'seqb'), split_axis=1, concat_axis=0, ti...  20.4 us
  transfers between devices with their start and end apart: 3, of which 3 were waited for; matrix products, arithmetic and copies ran while one was open for 9% of the time, Pallas kernels for 0%

commit v1 on v0

v1 whole, which is shorter than its diff:
```python
import functools
import math

import jax
import jax.numpy as jnp
import numpy as np
from jax import lax
from jax.experimental import pallas as pl
from jax.experimental.pallas import tpu as pltpu
from jax.sharding import PartitionSpec as P

MESH = pl.DeviceIdType.MESH
DOCS = 8
TOK, HEADS, WIDTH = 32, 128, 64
N, NB = 128, 8
HALF = TOK // 2
SUB = HALF // 2
TILES = 8
PER = N // TILES
SCALE = math.log2(math.e) / math.sqrt(WIDTH)
LOG_BASE = np.float32(-np.log(np.float32(10000.0)))
FREQS = [
    float(np.float32(np.exp(np.float64(np.float32(LOG_BASE * np.float32(i)) * 2.0 / WIDTH))))
    for i in range(WIDTH // 2)
]


def cos_sin(angle):
    turns = jnp.floor(angle * 0.6366197723675814 + 0.5)
    r = angle - turns * 1.5703125
    r = r - turns * 4.837512969970703125e-4
    r = r - turns * 7.54978995489188216e-8
    z = r * r
    s = ((-1.9515295891e-4 * z + 8.3321608736e-3) * z - 1.6666654611e-1) * z * r + r
    c = ((2.443315711809948e-5 * z - 1.388731625493765e-3) * z + 4.166664568298827e-2) * z * z
    c = c - 0.5 * z + 1.0
    quarter = turns.astype(jnp.int32)
    odd = (quarter & 1) == 1
    cosine = jnp.where(odd, s, c)
    sine = jnp.where(odd, c, s)
    cosine = jnp.where(((quarter + 1) & 2) == 2, -cosine, cosine)
    sine = jnp.where((quarter & 2) == 2, -sine, sine)
    return cosine, sine


def start_of(place, doc):
    start = jnp.zeros_like(place)
    for d in range(1, DOCS):
        start = jnp.where(place >= doc[d], doc[d], start)
    return start


def coords(p):
    return {"seqa": p // NB, "seqb": lax.rem(p, NB)}


def peer_of(me, m):
    zl, c, x, zh = me // 16, lax.rem(me // 8, 2), lax.rem(me // 2, 4), lax.rem(me, 2)
    k, r = lax.rem(m, 16), m // 16
    dz = jnp.where(lax.rem(k, 2) == 0, 16 - k // 2, (k + 1) // 2)
    z = lax.rem(zh * 8 + zl + dz, 16)
    x = lax.rem(x + r // 2, 4)
    c = lax.rem(c + r, 2)
    return ((lax.rem(z, 8) * 2 + c) * 4 + x) * 2 + z // 8


def kernel(
    q_hbm, k_hbm, v_hbm, doc_hbm, qg_hbm, kg_hbm, out_ref,
    qb, kb, vb, doc, gains, stage, send_a, send_b, recv_a, recv_b, vt, probs, kpos, wq,
    back, gathered, rows_out,
    in_sem, send_sem, ra_sem, rb_sem, back_send, back_recv,
):
    me = lax.axis_index("seqa") * NB + lax.axis_index("seqb")
    barrier = pltpu.get_barrier_semaphore()

    def greet(m, carry):
        p = lax.rem(me + m, N)
        pl.semaphore_signal(barrier, inc=1, device_id=coords(p), device_id_type=MESH)
        return carry

    lax.fori_loop(1, N, greet, 0)
    loads = [
        pltpu.make_async_copy(src, dst, in_sem.at[i])
        for i, (src, dst) in enumerate(
            (
                (doc_hbm, doc), (qg_hbm, gains.at[0]), (kg_hbm, gains.at[1]),
                (q_hbm, qb), (k_hbm, kb), (v_hbm, vb),
            )
        )
    ]
    for load in loads:
        load.start()
    for load in loads:
        load.wait()

    row = lax.broadcasted_iota(jnp.int32, (WIDTH // 2, HEADS), 0)
    freq = jnp.zeros((WIDTH // 2, HEADS), jnp.float32)
    for i, f in enumerate(FREQS):
        freq = jnp.where(row == i, jnp.float32(f), freq)
    gq, gk = (
        jnp.transpose(jnp.broadcast_to(gains[i], (HEADS, WIDTH)), (1, 0)) for i in range(2)
    )

    def prepared(x, gain, cosine, sine):
        x = x.astype(jnp.float32)
        mean = jnp.sum(x * x, axis=0, keepdims=True) * (1.0 / WIDTH)
        x = x * lax.rsqrt(mean + 1e-06) * gain
        a, b = x[: WIDTH // 2], x[WIDTH // 2 :]
        return a * cosine - b * sine, a * sine + b * cosine

    def pair_rows(r, carry):
        parts_q, parts_k, parts_v = [], [], []
        for t in (r, r + HALF):
            place = me * TOK + t
            pos = (place - start_of(place, doc)).astype(jnp.float32)
            cosine, sine = cos_sin(pos * freq)
            parts_q.extend(prepared(qb[t], gq, cosine, sine))
            parts_k.extend(prepared(kb[t], gk, cosine, sine))
            parts_v.append(vb[t].astype(jnp.float32))
        for at, parts in ((0, parts_k), (HALF, parts_v), (2 * HALF, parts_q)):
            block = jnp.transpose(jnp.concatenate(parts, axis=0), (1, 0))
            stage[pl.ds(at + r, HEADS, stride=3 * HALF), :] = block
        return carry

    lax.fori_loop(0, HALF, pair_rows, 0)

    def pack(h, carry):
        rows = stage[pl.ds(pl.multiple_of(h * 8 * 3 * HALF, 8), 8 * 3 * HALF), :]
        rows = rows.reshape(8, 3 * HALF, 2 * WIDTH)
        send_a[pl.ds(h * 8, 8)] = rows[:, : 2 * HALF + SUB].astype(jnp.bfloat16)
        send_b[pl.ds(h * 8, 8)] = rows[:, 2 * HALF + SUB :].astype(jnp.bfloat16)
        return carry

    lax.fori_loop(0, HEADS // 8, pack, 0)

    pl.semaphore_wait(barrier, N - 1)

    my_tile = me // PER

    def post_a(m, carry):
        p = peer_of(me, m)
        pltpu.make_async_remote_copy(
            src_ref=send_a.at[p], dst_ref=recv_a.at[me], send_sem=send_sem.at[0],
            recv_sem=ra_sem.at[my_tile], device_id=coords(p), device_id_type=MESH,
        ).start()
        return carry

    def post_b(m, carry):
        p = peer_of(me, m)
        pltpu.make_async_remote_copy(
            src_ref=send_b.at[p], dst_ref=recv_b.at[me], send_sem=send_sem.at[1],
            recv_sem=rb_sem.at[my_tile], device_id=coords(p), device_id_type=MESH,
        ).start()
        return carry

    lax.fori_loop(1, N, post_a, 0)
    lax.fori_loop(1, N, post_b, 0)
    own_a = pltpu.make_async_copy(send_a.at[me], recv_a.at[me], ra_sem.at[my_tile])
    own_b = pltpu.make_async_copy(send_b.at[me], recv_b.at[me], rb_sem.at[my_tile])
    own_a.start()
    own_b.start()

    key_row = lax.broadcasted_iota(jnp.int32, (PER * HALF, 2 * WIDTH), 0)
    kpos[...] = lax.rem(key_row, HALF) + (key_row // HALF) * TOK

    def arrived(ref, sem, j):
        part = ref.at[pl.ds(j * PER, PER)]
        pltpu.make_async_copy(part, part, sem.at[j]).wait()

    for j in range(TILES):
        arrived(recv_a, ra_sem, j)
    for j in range(TILES):
        v = recv_a[j * PER : (j + 1) * PER, HALF : 2 * HALF, :].reshape(PER * HALF, 2 * WIDTH)
        v = jnp.transpose(v.astype(jnp.float32), (1, 0)).astype(jnp.bfloat16)
        vt[j, :, : PER * HALF] = v[:WIDTH]
        vt[j, :, PER * HALF :] = v[WIDTH:]

    low = lax.broadcasted_iota(jnp.int32, (PER * SUB, 2 * WIDTH), 1) < WIDTH
    queries = 2 * PER * SUB
    span = PER * TOK

    def tile(i, g):
        if g == 0:
            x = recv_a[i * PER : (i + 1) * PER, 2 * HALF :, :]
        else:
            x = recv_b[i * PER : (i + 1) * PER]
        x = x.astype(jnp.float32).reshape(PER * SUB, 2 * WIDTH)
        turned = pltpu.roll(x, WIDTH, 1)
        zero = jnp.zeros_like(x)
        wq[0, : PER * SUB] = jnp.where(low, x, zero).astype(jnp.bfloat16)
        wq[0, PER * SUB :] = jnp.where(low, turned, zero).astype(jnp.bfloat16)
        wq[1, : PER * SUB] = jnp.where(low, zero, turned).astype(jnp.bfloat16)
        wq[1, PER * SUB :] = jnp.where(low, zero, x).astype(jnp.bfloat16)
        lane = lax.broadcasted_iota(jnp.int32, (1, queries), 1)
        within = lax.rem(lane, PER * SUB)
        place = (
            i * span + (within // SUB) * TOK + lax.rem(within, SUB) + g * SUB
            + jnp.where(lane >= PER * SUB, HALF, 0)
        )
        start = start_of(place, doc)
        total = jnp.zeros((8, queries), jnp.float32)
        for j in range(i + 1):
            keys = recv_a[j * PER : (j + 1) * PER, :HALF, :].reshape(PER * HALF, 2 * WIDTH)
            for half in range(2):
                scores = lax.dot_general(
                    keys, wq[half], (((1,), (1,)), ((), ())), preferred_element_type=jnp.float32
                )
                at = jnp.concatenate([kpos[...], kpos[...]], axis=1)
                base = j * span + half * HALF
                allowed = at >= start - base
                if j == i:
                    allowed = allowed & (at <= place - base)
                p = jnp.where(allowed, jnp.exp2(scores * SCALE), 0.0)
                probs[j, half * PER * HALF : (half + 1) * PER * HALF] = p
                total = total + jnp.sum(p.reshape(PER * HALF // 8, 8, queries), axis=0)
        inverse = 1.0 / jnp.sum(total, axis=0, keepdims=True)
        out = jnp.zeros((WIDTH, queries), jnp.float32)
        for j in range(i + 1):
            weights = (probs[j] * inverse).astype(jnp.bfloat16)
            out = out + jnp.dot(vt[j], weights, preferred_element_type=jnp.float32)
        out = jnp.concatenate([out[:, : PER * SUB], out[:, PER * SUB :]], axis=0)
        out = jnp.transpose(out, (1, 0)).reshape(PER, SUB, 2 * WIDTH)
        back[g, i * PER : (i + 1) * PER] = out.astype(jnp.bfloat16)

    def go_home(i, g):
        def one(s, carry):
            p = i * PER + s

            @pl.when(p != me)
            def _():
                pltpu.make_async_remote_copy(
                    src_ref=back.at[g, p], dst_ref=gathered.at[g, me], send_sem=back_send.at[g],
                    recv_sem=back_recv.at[g], device_id=coords(p), device_id_type=MESH,
                ).start()

            return carry

        lax.fori_loop(0, PER, one, 0)

    for g in range(2):
        if g == 1:
            for j in range(TILES):
                arrived(recv_b, rb_sem, j)

        def step(t, carry):
            i = lax.rem(my_tile + t, TILES)
            lax.switch(i, [functools.partial(tile, k, g) for k in range(TILES)])
            go_home(i, g)
            return carry

        lax.fori_loop(0, TILES, step, 0)

    def others(ref):
        part = ref.at[pl.ds(1, N - 1)]
        return part, part

    for g in range(2):
        gathered[g, me] = back[g, me]
        pltpu.make_async_copy(*others(gathered.at[g]), back_recv.at[g]).wait()
        rows_out[...] = gathered[g].astype(jnp.float32).reshape(HEADS * SUB, 2 * WIDTH)
        for r in range(SUB):
            block = jnp.transpose(rows_out[pl.ds(r, HEADS, stride=SUB), :], (1, 0))
            block = block.astype(jnp.bfloat16)
            out_ref[g * SUB + r] = block[:WIDTH]
            out_ref[g * SUB + r + HALF] = block[WIDTH:]
    pltpu.make_async_copy(*others(send_a), send_sem.at[0]).wait()
    pltpu.make_async_copy(*others(send_b), send_sem.at[1]).wait()
    for g in range(2):
        pltpu.make_async_copy(*others(back.at[g]), back_send.at[g]).wait()


def attention(queries, keys, values, doc_bounds, q_gain, k_gain):
    tok, heads, width = queries.shape
    assert (tok, heads, width) == (TOK, HEADS, WIDTH)
    queries, keys, values = (jnp.transpose(a, (0, 2, 1)) for a in (queries, keys, values))
    block = pltpu.VMEM((TOK, WIDTH, HEADS), jnp.bfloat16)
    bf16, f32 = jnp.bfloat16, jnp.float32
    dma = pltpu.SemaphoreType.DMA
    out = pl.pallas_call(
        kernel,
        out_shape=jax.ShapeDtypeStruct((TOK, WIDTH, HEADS), bf16),
        in_specs=[pl.BlockSpec(memory_space=pl.ANY)] * 6,
        out_specs=pl.BlockSpec(memory_space=pltpu.VMEM),
        scratch_shapes=[
            block, block, block,
            pltpu.SMEM(doc_bounds.shape, jnp.int32),
            pltpu.VMEM((2, 1, WIDTH), f32),
            pltpu.VMEM((HEADS * 3 * HALF, 2 * WIDTH), f32),
            pltpu.VMEM((N, 2 * HALF + SUB, 2 * WIDTH), bf16),
            pltpu.VMEM((N, SUB, 2 * WIDTH), bf16),
            pltpu.VMEM((N, 2 * HALF + SUB, 2 * WIDTH), bf16),
            pltpu.VMEM((N, SUB, 2 * WIDTH), bf16),
            pltpu.VMEM((TILES, WIDTH, 2 * PER * HALF), bf16),
            pltpu.VMEM((TILES, 2 * PER * HALF, 2 * PER * SUB), f32),
            pltpu.VMEM((PER * HALF, 2 * WIDTH), jnp.int32),
            pltpu.VMEM((2, 2 * PER * SUB, 2 * WIDTH), bf16),
            pltpu.VMEM((2, N, SUB, 2 * WIDTH), bf16),
            pltpu.VMEM((2, N, SUB, 2 * WIDTH), bf16),
            pltpu.VMEM((HEADS * SUB, 2 * WIDTH), f32),
            dma((6,)), dma((2,)), dma((TILES,)), dma((TILES,)), dma((2,)), dma((2,)),
        ],
        compiler_params=pltpu.CompilerParams(
            collective_id=0, has_side_effects=True, vmem_limit_bytes=60 << 20
        ),
    )(queries, keys, values, doc_bounds, q_gain.reshape(1, WIDTH), k_gain.reshape(1, WIDTH))
    return jnp.transpose(out, (0, 2, 1))


def solution(mesh):
    assert mesh.shape["seqa"] * mesh.shape["seqb"] == N and mesh.shape["seqb"] == NB
    rows = P(("dp", "seqa", "seqb"), None, None)
    return jax.shard_map(
        attention,
        mesh=mesh,
        in_specs=(rows, rows, rows, P("dp"), P(), P()),
        out_specs=rows,
        check_vma=False,
    )
```

time: 309 us -> 135 us (0.44)
  the two profiles are of different devices: /device:TPU:1 before, /device:TPU:143 now
where the time goes in v1:
time: 135 us
  Pallas kernels  133 us (99%)
  local copies, waits for them, and re-layouts  1.87 us (1%)
    pallas_call x1, Pallas kernels, attention(): pl.pallas_call(kernel, out_shape=jax.ShapeDtypeStruct((TOK, WIDTH, HEADS)...  133 us

profile of v1, /device:TPU:143, one launch (start us, length us, event | category | flops | bytes accessed | tf_op | source)
XLA Modules:
  0.0 134.6 jit_solution(9508334879044342980)
XLA Ops:
  0.0 132.7 %shard_map.64 = bf16[32,64,128]{2,1,0:T(8,128)(2,1)} custom-call(bf16[32,64,128]{2,1,0:T(8,128)(2,1)} %bitcast.7, bf16[32,64,128]{2,1,0:T(8,128)(2,1)} %bitcast.8, bf16[32,64,128]{2,1,0:T(8,128)(2,1)} %bitcast.9, s32[9]{0:T(128)} %doc_hbm.1, f32[1,64]{1,0:T(1,128)} %bitcast.10, f32[1,64]{1,0:T(1,128)} %bitcast.11), custom_call_target="tpu_custom_call" | custom-call | tf_op jit(solution)/shard_map/pallas_call | solution.py:279
  132.8 1.9 %copy.8 = bf16[32,128,64]{1,2,0:T(8,128)(2,1)} copy(bf16[32,128,64]{1,2,0:T(8,128)(2,1)} %bitcast.6) | data formatting | bytes 1048576

commit v2 on v1

--- a/solution.py
+++ b/solution.py
@@ -50,56 +50,57 @@
     return start
 
 
-def coords(p):
-    return {"seqa": p // NB, "seqb": lax.rem(p, NB)}
-
-
-def peer_of(me, m):
-    zl, c, x, zh = me // 16, lax.rem(me // 8, 2), lax.rem(me // 2, 4), lax.rem(me, 2)
-    k, r = lax.rem(m, 16), m // 16
-    dz = jnp.where(lax.rem(k, 2) == 0, 16 - k // 2, (k + 1) // 2)
-    z = lax.rem(zh * 8 + zl + dz, 16)
-    x = lax.rem(x + r // 2, 4)
-    c = lax.rem(c + r, 2)
-    return ((lax.rem(z, 8) * 2 + c) * 4 + x) * 2 + z // 8
-
-
 def kernel(
     q_hbm, k_hbm, v_hbm, doc_hbm, qg_hbm, kg_hbm, out_ref,
     qb, kb, vb, doc, gains, stage, send_a, send_b, recv_a, recv_b, vt, probs, kpos, wq,
     back, gathered, rows_out,
-    in_sem, send_sem, ra_sem, rb_sem, back_send, back_recv,
+    in_sem, send_sem, ra_sem, rb_sem, back_send, back_recv, from_below, from_above,
 ):
-    me = lax.axis_index("seqa") * NB + lax.axis_index("seqb")
-    barrier = pltpu.get_barrier_semaphore()
-
-    def greet(m, carry):
-        p = lax.rem(me + m, N)
-        pl.semaphore_signal(barrier, inc=1, device_id=coords(p), device_id_type=MESH)
-        return carry
-
-    lax.fori_loop(1, N, greet, 0)
-    loads = [
-        pltpu.make_async_copy(src, dst, in_sem.at[i])
-        for i, (src, dst) in enumerate(
-            (
-                (doc_hbm, doc), (qg_hbm, gains.at[0]), (kg_hbm, gains.at[1]),
-                (q_hbm, qb), (k_hbm, kb), (v_hbm, vb),
+    seqa, seqb = lax.axis_index("seqa"), lax.axis_index("seqb")
+    me = seqa * NB + seqb
+    my_tile = seqa // 2
+    core, chip_x, chip_z = lax.rem(seqa, 2), seqb // 2, lax.rem(seqb, 2) * 8 + my_tile
+    across = [(chip_x, core)] + [
+        (lax.rem(chip_x + i // 2, 4), lax.rem(core + i, 2)) for i in range(1, 8)
+    ]
+
+    def at_plane(z):
+        z = lax.rem(z, 16)
+        low, high = lax.rem(z, 8), z // 8
+        return [
+            (low * 16 + c * 8 + x * 2 + high, {"seqa": low * 2 + c, "seqb": x * 2 + high})
+            for x, c in across
+        ]
+
+    with jax.named_scope("greet"):
+        loads = [
+            pltpu.make_async_copy(src, dst, in_sem.at[i])
+            for i, (src, dst) in enumerate(
+                (
+                    (doc_hbm, doc), (qg_hbm, gains.at[0]), (kg_hbm, gains.at[1]),
+                    (q_hbm, qb), (k_hbm, kb), (v_hbm, vb),
+                )
             )
-        )
-    ]
-    for load in loads:
-        load.start()
-    for load in loads:
-        load.wait()
+        ]
+        for load in loads:
+            load.start()
+        barrier = pltpu.get_barrier_semaphore()
+        above, below = at_plane(chip_z + 1)[0][1], at_plane(chip_z + 15)[0][1]
+        for where in [at[1] for at in at_plane(chip_z)[1:]] + [above, below]:
+            pl.semaphore_signal(barrier, inc=1, device_id=where, device_id_type=MESH)
 
     row = lax.broadcasted_iota(jnp.int32, (WIDTH // 2, HEADS), 0)
     freq = jnp.zeros((WIDTH // 2, HEADS), jnp.float32)
     for i, f in enumerate(FREQS):
         freq = jnp.where(row == i, jnp.float32(f), freq)
+    with jax.named_scope("load"):
+        for load in loads:
+            load.wait()
     gq, gk = (
         jnp.transpose(jnp.broadcast_to(gains[i], (HEADS, WIDTH)), (1, 0)) for i in range(2)
     )
+    place = me * TOK + lax.broadcasted_iota(jnp.int32, (1, HEADS), 1)
+    cosines, sines = cos_sin((place - start_of(place, doc)).astype(jnp.float32) * freq)
 
     def prepared(x, gain, cosine, sine):
         x = x.astype(jnp.float32)
@@ -108,21 +109,20 @@
         a, b = x[: WIDTH // 2], x[WIDTH // 2 :]
         return a * cosine - b * sine, a * sine + b * cosine
 
-    def pair_rows(r, carry):
-        parts_q, parts_k, parts_v = [], [], []
-        for t in (r, r + HALF):
-            place = me * TOK + t
-            pos = (place - start_of(place, doc)).astype(jnp.float32)
-            cosine, sine = cos_sin(pos * freq)
-            parts_q.extend(prepared(qb[t], gq, cosine, sine))
-            parts_k.extend(prepared(kb[t], gk, cosine, sine))
-            parts_v.append(vb[t].astype(jnp.float32))
-        for at, parts in ((0, parts_k), (HALF, parts_v), (2 * HALF, parts_q)):
-            block = jnp.transpose(jnp.concatenate(parts, axis=0), (1, 0))
-            stage[pl.ds(at + r, HEADS, stride=3 * HALF), :] = block
-        return carry
-
-    lax.fori_loop(0, HALF, pair_rows, 0)
+    with jax.named_scope("prep"):
+        for r in range(HALF):
+            parts_q, parts_k, parts_v = [], [], []
+            for t in (r, r + HALF):
+                cosine, sine = (
+                    jnp.broadcast_to(table[:, t : t + 1], (WIDTH // 2, HEADS))
+                    for table in (cosines, sines)
+                )
+                parts_q.extend(prepared(qb[t], gq, cosine, sine))
+                parts_k.extend(prepared(kb[t], gk, cosine, sine))
+                parts_v.append(vb[t].astype(jnp.float32))
+            for at, parts in ((0, parts_k), (HALF, parts_v), (2 * HALF, parts_q)):
+                block = jnp.transpose(jnp.concatenate(parts, axis=0), (1, 0))
+                stage[pl.ds(at + r, HEADS, stride=3 * HALF), :] = block
 
     def pack(h, carry):
         rows = stage[pl.ds(pl.multiple_of(h * 8 * 3 * HALF, 8), 8 * 3 * HALF), :]
@@ -131,35 +131,75 @@
         send_b[pl.ds(h * 8, 8)] = rows[:, 2 * HALF + SUB :].astype(jnp.bfloat16)
         return carry
 
-    lax.fori_loop(0, HEADS // 8, pack, 0)
-
-    pl.semaphore_wait(barrier, N - 1)
-
-    my_tile = me // PER
-
-    def post_a(m, carry):
-        p = peer_of(me, m)
+    with jax.named_scope("pack"):
+        lax.fori_loop(0, HEADS // 8, pack, 0)
+
+    def post(which, p, where):
+        source, target, arrival = (
+            (send_a, recv_a, ra_sem), (send_b, recv_b, rb_sem)
+        )[which]
         pltpu.make_async_remote_copy(
-            src_ref=send_a.at[p], dst_ref=recv_a.at[me], send_sem=send_sem.at[0],
-            recv_sem=ra_sem.at[my_tile], device_id=coords(p), device_id_type=MESH,
+            src_ref=source.at[p], dst_ref=target.at[me], send_sem=send_sem.at[which],
+            recv_sem=arrival.at[my_tile], device_id=where, device_id_type=MESH,
         ).start()
-        return carry
-
-    def post_b(m, carry):
-        p = peer_of(me, m)
-        pltpu.make_async_remote_copy(
-            src_ref=send_b.at[p], dst_ref=recv_b.at[me], send_sem=send_sem.at[1],
-            recv_sem=rb_sem.at[my_tile], device_id=coords(p), device_id_type=MESH,
-        ).start()
-        return carry
-
-    lax.fori_loop(1, N, post_a, 0)
-    lax.fori_loop(1, N, post_b, 0)
+
+    def post_mixed(which, spots):
+        for i in spots:
+            x, c = across[i]
+
+            def one(k, carry):
+                away = jnp.where(lax.rem(k, 2) == 1, 8 - (k + 1) // 2, 8 + k // 2)
+                z = lax.rem(chip_z + away, 16)
+                low, high = lax.rem(z, 8), z // 8
+                post(
+                    which, low * 16 + c * 8 + x * 2 + high,
+                    {"seqa": low * 2 + c, "seqb": x * 2 + high},
+                )
+                return carry
+
+            lax.fori_loop(0, 15 if i == 0 else 16, one, 0)
+
+    def tell(sem, where):
+        pl.semaphore_signal(sem, inc=1, device_id=where, device_id_type=MESH)
+
+    with jax.named_scope("barrier"):
+        pl.semaphore_wait(barrier, 9)
+    near = 4
+    with jax.named_scope("post_a"):
+        tell(from_below.at[1], above)
+        tell(from_above.at[1], below)
+        for at in at_plane(chip_z)[1:near]:
+            post(0, *at)
+
+        def ring(k, carry):
+            pl.semaphore_wait(from_below.at[k], 1)
+            tell(from_below.at[k + 1], above)
+            pl.semaphore_wait(from_above.at[k], 1)
+
+            @pl.when(k < 7)
+            def _():
+                tell(from_above.at[k + 1], below)
+
+            for at in at_plane(chip_z + 16 - k)[:near] + at_plane(chip_z + k)[:near]:
+                post(0, *at)
+            return carry
+
+        lax.fori_loop(1, 8, ring, 0)
+        pl.semaphore_wait(from_below.at[8], 1)
+        for at in at_plane(chip_z + 8)[:near]:
+            post(0, *at)
+        post_mixed(0, range(near, 8))
+    with jax.named_scope("post_b"):
+        post_mixed(1, range(8))
     own_a = pltpu.make_async_copy(send_a.at[me], recv_a.at[me], ra_sem.at[my_tile])
     own_b = pltpu.make_async_copy(send_b.at[me], recv_b.at[me], rb_sem.at[my_tile])
     own_a.start()
     own_b.start()
 
+    def others(ref):
+        part = ref.at[pl.ds(1, N - 1)]
+        return part, part
+
     key_row = lax.broadcasted_iota(jnp.int32, (PER * HALF, 2 * WIDTH), 0)
     kpos[...] = lax.rem(key_row, HALF) + (key_row // HALF) * TOK
 
@@ -167,8 +207,9 @@
         part = ref.at[pl.ds(j * PER, PER)]
         pltpu.make_async_copy(part, part, sem.at[j]).wait()
 
-    for j in range(TILES):
-        arrived(recv_a, ra_sem, j)
+    with jax.named_scope("wait_a"):
+        for j in range(TILES):
+            arrived(recv_a, ra_sem, j)
     for j in range(TILES):
         v = recv_a[j * PER : (j + 1) * PER, HALF : 2 * HALF, :].reshape(PER * HALF, 2 * WIDTH)
         v = jnp.transpose(v.astype(jnp.float32), (1, 0)).astype(jnp.bfloat16)
@@ -221,42 +262,34 @@
         out = jnp.concatenate([out[:, : PER * SUB], out[:, PER * SUB :]], axis=0)
         out = jnp.transpose(out, (1, 0)).reshape(PER, SUB, 2 * WIDTH)
         back[g, i * PER : (i + 1) * PER] = out.astype(jnp.bfloat16)
-
-    def go_home(i, g):
-        def one(s, carry):
-            p = i * PER + s
+        for p in range(i * PER, (i + 1) * PER):
 
             @pl.when(p != me)
             def _():
                 pltpu.make_async_remote_copy(
                     src_ref=back.at[g, p], dst_ref=gathered.at[g, me], send_sem=back_send.at[g],
-                    recv_sem=back_recv.at[g], device_id=coords(p), device_id_type=MESH,
+                    recv_sem=back_recv.at[g], device_id={"seqa": p // NB, "seqb": p % NB},
+                    device_id_type=MESH,
                 ).start()
-
-            return carry
-
-        lax.fori_loop(0, PER, one, 0)
 
     for g in range(2):
         if g == 1:
-            for j in range(TILES):
-                arrived(recv_b, rb_sem, j)
+            with jax.named_scope("wait_b"):
+                for j in range(TILES):
+                    arrived(recv_b, rb_sem, j)
 
         def step(t, carry):
-            i = lax.rem(my_tile + t, TILES)
+            i = lax.rem(my_tile + jnp.where(lax.rem(t, 2) == 1, TILES - (t + 1) // 2, t // 2), TILES)
             lax.switch(i, [functools.partial(tile, k, g) for k in range(TILES)])
-            go_home(i, g)
             return carry
 
-        lax.fori_loop(0, TILES, step, 0)
-
-    def others(ref):
-        part = ref.at[pl.ds(1, N - 1)]
-        return part, part
+        with jax.named_scope(f"tiles_{g}"):
+            lax.fori_loop(0, TILES, step, 0)
 
     for g in range(2):
         gathered[g, me] = back[g, me]
-        pltpu.make_async_copy(*others(gathered.at[g]), back_recv.at[g]).wait()
+        with jax.named_scope(f"wait_back_{g}"):
+            pltpu.make_async_copy(*others(gathered.at[g]), back_recv.at[g]).wait()
         rows_out[...] = gathered[g].astype(jnp.float32).reshape(HEADS * SUB, 2 * WIDTH)
         for r in range(SUB):
             block = jnp.transpose(rows_out[pl.ds(r, HEADS, stride=SUB), :], (1, 0))
@@ -298,6 +331,7 @@
             pltpu.VMEM((2, N, SUB, 2 * WIDTH), bf16),
             pltpu.VMEM((HEADS * SUB, 2 * WIDTH), f32),
             dma((6,)), dma((2,)), dma((TILES,)), dma((TILES,)), dma((2,)), dma((2,)),
+            pltpu.SemaphoreType.REGULAR((9,)), pltpu.SemaphoreType.REGULAR((8,)),
         ],
         compiler_params=pltpu.CompilerParams(
             collective_id=0, has_side_effects=True, vmem_limit_bytes=60 << 20

time: 135 us -> 117 us (0.87)
  the two profiles are of different devices: /device:TPU:143 before, /device:TPU:1 now
where the time goes in v2:
time: 117 us
  Pallas kernels  115 us (98%)
  local copies, waits for them, and re-layouts  1.87 us (2%)
    pallas_call x1, Pallas kernels, attention(): pl.pallas_call(kernel, out_shape=jax.ShapeDtypeStruct((TOK, WIDTH, HEADS)...  115 us

profile of v2, /device:TPU:1, one launch (start us, length us, event | category | flops | bytes accessed | tf_op | source)
XLA Modules:
  0.0 116.9 jit_solution(13046750673070689092)
XLA Ops:
  0.0 115.0 %shard_map.64 = bf16[32,64,128]{2,1,0:T(8,128)(2,1)} custom-call(bf16[32,64,128]{2,1,0:T(8,128)(2,1)} %bitcast.7, bf16[32,64,128]{2,1,0:T(8,128)(2,1)} %bitcast.8, bf16[32,64,128]{2,1,0:T(8,128)(2,1)} %bitcast.9, s32[9]{0:T(128)} %doc_hbm.1, f32[1,64]{1,0:T(1,128)} %bitcast.10, f32[1,64]{1,0:T(1,128)} %bitcast.11), custom_call_target="tpu_custom_call" | custom-call | tf_op jit(solution)/shard_map/pallas_call | solution.py:312
  115.0 1.9 %copy.8 = bf16[32,128,64]{1,2,0:T(8,128)(2,1)} copy(bf16[32,128,64]{1,2,0:T(8,128)(2,1)} %bitcast.6) | data formatting | bytes 1048576

commit v3 on v2

--- a/solution.py
+++ b/solution.py
@@ -17,6 +17,7 @@
 SUB = HALF // 2
 TILES = 8
 PER = N // TILES
+FAR = -2048.0
 SCALE = math.log2(math.e) / math.sqrt(WIDTH)
 LOG_BASE = np.float32(-np.log(np.float32(10000.0)))
 FREQS = [
@@ -52,8 +53,8 @@
 
 def kernel(
     q_hbm, k_hbm, v_hbm, doc_hbm, qg_hbm, kg_hbm, out_ref,
-    qb, kb, vb, doc, gains, stage, send_a, send_b, recv_a, recv_b, vt, probs, kpos, wq,
-    back, gathered, rows_out,
+    qb, kb, vb, doc, gains, stage, send_a, send_b, recv_a, recv_b, kx, vt, probs_a, probs_b, kpos, qpos,
+    wq,    back, gathered, rows_out,
     in_sem, send_sem, ra_sem, rb_sem, back_send, back_recv, from_below, from_above,
 ):
     seqa, seqb = lax.axis_index("seqa"), lax.axis_index("seqb")
@@ -200,61 +201,78 @@
         part = ref.at[pl.ds(1, N - 1)]
         return part, part
 
-    key_row = lax.broadcasted_iota(jnp.int32, (PER * HALF, 2 * WIDTH), 0)
+    def arrived(ref, sem, j):
+        part = ref.at[pl.ds(pl.multiple_of(j * PER, PER), PER)]
+        pltpu.make_async_copy(part, part, sem.at[j]).wait()
+
+    queries, span, keys = 2 * PER * SUB, PER * TOK, PER * HALF
+    lane = lax.broadcasted_iota(jnp.int32, (1, 2 * WIDTH), 1)
+    mark = lax.rem(lane, WIDTH)
+    first_of, end_of = jnp.full_like(lane, TILES * span), jnp.zeros_like(lane)
+    for d in range(DOCS):
+        first_of = jnp.where(mark == d, doc[d], first_of)
+        end_of = jnp.where(mark == d, doc[d + 1], end_of)
+    low = lane < WIDTH
+    key_row = lax.broadcasted_iota(jnp.int32, (keys, 2 * WIDTH), 0)
     kpos[...] = lax.rem(key_row, HALF) + (key_row // HALF) * TOK
-
-    def arrived(ref, sem, j):
-        part = ref.at[pl.ds(j * PER, PER)]
-        pltpu.make_async_copy(part, part, sem.at[j]).wait()
-
-    with jax.named_scope("wait_a"):
-        for j in range(TILES):
-            arrived(recv_a, ra_sem, j)
-    for j in range(TILES):
-        v = recv_a[j * PER : (j + 1) * PER, HALF : 2 * HALF, :].reshape(PER * HALF, 2 * WIDTH)
+    query_row = lax.broadcasted_iota(jnp.int32, (PER * SUB, 2 * WIDTH), 0)
+    qpos[...] = lax.rem(query_row, SUB) + (query_row // SUB) * TOK
+
+    def marks(at, same, other):
+        return jnp.where((at >= first_of) & (at < end_of), same, other)
+
+    def take_keys(j):
+        both = recv_a[pl.ds(j * PER, PER), : 2 * HALF, :]
+        k = both[:, :HALF].reshape(keys, 2 * WIDTH)
+        one, zero = jnp.float32(1.0), jnp.float32(0.0)
+        for half in range(2):
+            own = low if half == 0 else jnp.logical_not(low)
+            at = kpos[...] + (j * span + half * HALF)
+            marked = jnp.where(own, k.astype(jnp.float32), marks(at, one, zero))
+            kx[half, j] = marked.astype(jnp.bfloat16)
+        v = both[:, HALF:].reshape(keys, 2 * WIDTH)
         v = jnp.transpose(v.astype(jnp.float32), (1, 0)).astype(jnp.bfloat16)
-        vt[j, :, : PER * HALF] = v[:WIDTH]
-        vt[j, :, PER * HALF :] = v[WIDTH:]
-
-    low = lax.broadcasted_iota(jnp.int32, (PER * SUB, 2 * WIDTH), 1) < WIDTH
-    queries = 2 * PER * SUB
-    span = PER * TOK
-
-    def tile(i, g):
+        vt[j, :, :keys] = v[:WIDTH]
+        vt[j, :, keys:] = v[WIDTH:]
+
+    def take_queries(i, g):
         if g == 0:
-            x = recv_a[i * PER : (i + 1) * PER, 2 * HALF :, :]
+            x = recv_a[pl.ds(i * PER, PER), 2 * HALF :, :]
         else:
-            x = recv_b[i * PER : (i + 1) * PER]
+            x = recv_b[pl.ds(i * PER, PER)]
         x = x.astype(jnp.float32).reshape(PER * SUB, 2 * WIDTH)
         turned = pltpu.roll(x, WIDTH, 1)
-        zero = jnp.zeros_like(x)
-        wq[0, : PER * SUB] = jnp.where(low, x, zero).astype(jnp.bfloat16)
-        wq[0, PER * SUB :] = jnp.where(low, turned, zero).astype(jnp.bfloat16)
-        wq[1, : PER * SUB] = jnp.where(low, zero, turned).astype(jnp.bfloat16)
-        wq[1, PER * SUB :] = jnp.where(low, zero, x).astype(jnp.bfloat16)
-        lane = lax.broadcasted_iota(jnp.int32, (1, queries), 1)
-        within = lax.rem(lane, PER * SUB)
+        for late in range(2):
+            at = qpos[...] + (i * span + g * SUB + late * HALF)
+            m = marks(at, jnp.float32(0.0), jnp.float32(FAR))
+            rows = pl.ds(late * PER * SUB, PER * SUB)
+            first, second = (x, turned) if late == 0 else (turned, x)
+            wq[0, i, rows] = jnp.where(low, first, m).astype(jnp.bfloat16)
+            wq[1, i, rows] = jnp.where(low, m, second).astype(jnp.bfloat16)
+
+    def scores_of(i, g, probs):
+        spot = lax.broadcasted_iota(jnp.int32, (1, queries), 1)
+        within = lax.rem(spot, PER * SUB)
         place = (
-            i * span + (within // SUB) * TOK + lax.rem(within, SUB) + g * SUB
-            + jnp.where(lane >= PER * SUB, HALF, 0)
+            (within // SUB) * TOK + lax.rem(within, SUB) + g * SUB
+            + jnp.where(spot >= PER * SUB, HALF, 0)
         )
-        start = start_of(place, doc)
-        total = jnp.zeros((8, queries), jnp.float32)
+        total = jnp.zeros((16, queries), jnp.float32)
         for j in range(i + 1):
-            keys = recv_a[j * PER : (j + 1) * PER, :HALF, :].reshape(PER * HALF, 2 * WIDTH)
             for half in range(2):
-                scores = lax.dot_general(
-                    keys, wq[half], (((1,), (1,)), ((), ())), preferred_element_type=jnp.float32
+                p = lax.dot_general(
+                    kx[half, j], wq[half, i], (((1,), (1,)), ((), ())),
+                    preferred_element_type=jnp.float32,
                 )
-                at = jnp.concatenate([kpos[...], kpos[...]], axis=1)
-                base = j * span + half * HALF
-                allowed = at >= start - base
+                p = jnp.exp2(p * SCALE)
                 if j == i:
-                    allowed = allowed & (at <= place - base)
-                p = jnp.where(allowed, jnp.exp2(scores * SCALE), 0.0)
-                probs[j, half * PER * HALF : (half + 1) * PER * HALF] = p
-                total = total + jnp.sum(p.reshape(PER * HALF // 8, 8, queries), axis=0)
-        inverse = 1.0 / jnp.sum(total, axis=0, keepdims=True)
+                    at = jnp.concatenate([kpos[...], kpos[...]], axis=1)
+                    p = jnp.where(at <= place - half * HALF, p, 0.0)
+                probs[j, half * keys : (half + 1) * keys] = p
+                total = total + jnp.sum(p.reshape(keys // 16, 16, queries), axis=0)
+        return 1.0 / jnp.sum(total, axis=0, keepdims=True)
+
+    def outputs_of(i, g, probs, inverse):
         out = jnp.zeros((WIDTH, queries), jnp.float32)
         for j in range(i + 1):
             weights = (probs[j] * inverse).astype(jnp.bfloat16)
@@ -262,29 +280,65 @@
         out = jnp.concatenate([out[:, : PER * SUB], out[:, PER * SUB :]], axis=0)
         out = jnp.transpose(out, (1, 0)).reshape(PER, SUB, 2 * WIDTH)
         back[g, i * PER : (i + 1) * PER] = out.astype(jnp.bfloat16)
-        for p in range(i * PER, (i + 1) * PER):
-
-            @pl.when(p != me)
-            def _():
-                pltpu.make_async_remote_copy(
-                    src_ref=back.at[g, p], dst_ref=gathered.at[g, me], send_sem=back_send.at[g],
-                    recv_sem=back_recv.at[g], device_id={"seqa": p // NB, "seqb": p % NB},
-                    device_id_type=MESH,
-                ).start()
+
+    def send_home(i, g, high, c, x):
+        p = i * PER + c * NB + x * 2 + high
+
+        @pl.when(p != me)
+        def _():
+            pltpu.make_async_remote_copy(
+                src_ref=back.at[g, p], dst_ref=gathered.at[g, me], send_sem=back_send.at[g],
+                recv_sem=back_recv.at[g], device_id={"seqa": 2 * i + c, "seqb": x * 2 + high},
+                device_id_type=MESH,
+            ).start()
+
+    def pair(first, g):
+        second = first + TILES // 2
+        small = scores_of(first, g, probs_a)
+        large = scores_of(second, g, probs_b)
+        outputs_of(first, g, probs_a, small)
+        outputs_of(second, g, probs_b, large)
+        for c in range(2):
+            for x in range(4):
+                send_home(first, g, 0, c, x)
+                send_home(second, g, 0, c, x)
+
+    def late_half(t, g):
+        i = lax.rem(my_tile + jnp.where(lax.rem(t, 2) == 1, TILES - (t + 1) // 2, t // 2), TILES)
+        for c in range(2):
+            for x in range(4):
+                send_home(i, g, 1, c, x)
+
+    def come_in(j, carry):
+        arrived(recv_a, ra_sem, j)
+        take_keys(j)
+        take_queries(j, 0)
+        return carry
+
+    def come_in_b(j, carry):
+        arrived(recv_b, rb_sem, j)
+        take_queries(j, 1)
+        return carry
 
     for g in range(2):
-        if g == 1:
-            with jax.named_scope("wait_b"):
-                for j in range(TILES):
-                    arrived(recv_b, rb_sem, j)
+        with jax.named_scope(f"wait_{g}"):
+            lax.fori_loop(0, TILES, come_in if g == 0 else come_in_b, 0)
 
         def step(t, carry):
-            i = lax.rem(my_tile + jnp.where(lax.rem(t, 2) == 1, TILES - (t + 1) // 2, t // 2), TILES)
-            lax.switch(i, [functools.partial(tile, k, g) for k in range(TILES)])
+            away = jnp.where(t >= 2, 5 - t, t)
+            i = lax.rem(my_tile + away, TILES // 2)
+            lax.switch(i, [functools.partial(pair, k, g) for k in range(TILES // 2)])
             return carry
 
         with jax.named_scope(f"tiles_{g}"):
-            lax.fori_loop(0, TILES, step, 0)
+            lax.fori_loop(0, TILES // 2, step, 0)
+
+        def rest(t, carry):
+            late_half(t, g)
+            return carry
+
+        with jax.named_scope(f"rest_{g}"):
+            lax.fori_loop(0, TILES, rest, 0)
 
     for g in range(2):
         gathered[g, me] = back[g, me]
@@ -311,7 +365,7 @@
     dma = pltpu.SemaphoreType.DMA
     out = pl.pallas_call(
         kernel,
-        out_shape=jax.ShapeDtypeStruct((TOK, WIDTH, HEADS), bf16),
+        out_shape=pltpu.VMEM((TOK, WIDTH, HEADS), bf16),
         in_specs=[pl.BlockSpec(memory_space=pl.ANY)] * 6,
         out_specs=pl.BlockSpec(memory_space=pltpu.VMEM),
         scratch_shapes=[
@@ -323,10 +377,13 @@
             pltpu.VMEM((N, SUB, 2 * WIDTH), bf16),
             pltpu.VMEM((N, 2 * HALF + SUB, 2 * WIDTH), bf16),
             pltpu.VMEM((N, SUB, 2 * WIDTH), bf16),
+            pltpu.VMEM((2, TILES, PER * HALF, 2 * WIDTH), bf16),
             pltpu.VMEM((TILES, WIDTH, 2 * PER * HALF), bf16),
+            pltpu.VMEM((TILES // 2, 2 * PER * HALF, 2 * PER * SUB), f32),
             pltpu.VMEM((TILES, 2 * PER * HALF, 2 * PER * SUB), f32),
             pltpu.VMEM((PER * HALF, 2 * WIDTH), jnp.int32),
-            pltpu.VMEM((2, 2 * PER * SUB, 2 * WIDTH), bf16),
+            pltpu.VMEM((PER * SUB, 2 * WIDTH), jnp.int32),
+            pltpu.VMEM((2, TILES, 2 * PER * SUB, 2 * WIDTH), bf16),
             pltpu.VMEM((2, N, SUB, 2 * WIDTH), bf16),
             pltpu.VMEM((2, N, SUB, 2 * WIDTH), bf16),
             pltpu.VMEM((HEADS * SUB, 2 * WIDTH), f32),

time: 117 us -> 111 us (0.949)
  Pallas kernels: 115 us -> 110 us
    pallas_call x1, Pallas kernels: 115 us -> 110 us  [attention(): pl.pallas_call(kernel, out_shape=pltpu.VMEM((TOK, WIDTH, HEADS), bf16), i...]
where the time goes in v3:
time: 111 us
  Pallas kernels  110 us (99%)
    pallas_call x1, Pallas kernels, attention(): pl.pallas_call(kernel, out_shape=pltpu.VMEM((TOK, WIDTH, HEADS), bf16), i...  110 us

profile of v3, /device:TPU:1, one launch (start us, length us, event | category | flops | bytes accessed | tf_op | source)
XLA Modules:
  0.0 111.0 jit_solution(17988518666768850335)
XLA Ops:
  0.0 110.2 %shard_map.64 = bf16[32,64,128]{2,1,0:T(8,128)(2,1)S(1)} custom-call(bf16[32,64,128]{2,1,0:T(8,128)(2,1)} %bitcast.7, bf16[32,64,128]{2,1,0:T(8,128)(2,1)} %bitcast.8, bf16[32,64,128]{2,1,0:T(8,128)(2,1)} %bitcast.9, s32[9]{0:T(128)} %doc_hbm.1, f32[1,64]{1,0:T(1,128)} %bitcast.10, f32[1,64]{1,0:T(1,128)} %bitcast.11), custom_call_target="tpu_custom_call" | custom-call | tf_op jit(solution)/shard_map/pallas_call | solution.py:366
  110.2 0.8 copy.8

commit v4 on v3

--- a/solution.py
+++ b/solution.py
@@ -325,8 +325,10 @@
             lax.fori_loop(0, TILES, come_in if g == 0 else come_in_b, 0)
 
         def step(t, carry):
-            away = jnp.where(t >= 2, 5 - t, t)
-            i = lax.rem(my_tile + away, TILES // 2)
+            m = lax.rem(my_tile, TILES // 2)
+            second = jnp.where(m == 0, 1, 0)
+            third = jnp.where(m == 0, 2, jnp.where(m == 3, 1, 3))
+            i = jnp.where(t == 0, m, jnp.where(t == 1, second, jnp.where(t == 2, third, 6 - m - second - third)))
             lax.switch(i, [functools.partial(pair, k, g) for k in range(TILES // 2)])
             return carry
 

time: 111 us -> 111 us (level)
  no operation moved by 1% of the time
where the time goes in v4:
time: 111 us
  Pallas kernels  110 us (99%)
    pallas_call x1, Pallas kernels, attention(): pl.pallas_call(kernel, out_shape=pltpu.VMEM((TOK, WIDTH, HEADS), bf16), i...  110 us

profile of v4, /device:TPU:1, one launch (start us, length us, event | category | flops | bytes accessed | tf_op | source)
XLA Modules:
  0.0 110.8 jit_solution(13222652869979029162)
XLA Ops:
  0.0 110.0 %shard_map.64 = bf16[32,64,128]{2,1,0:T(8,128)(2,1)S(1)} custom-call(bf16[32,64,128]{2,1,0:T(8,128)(2,1)} %bitcast.7, bf16[32,64,128]{2,1,0:T(8,128)(2,1)} %bitcast.8, bf16[32,64,128]{2,1,0:T(8,128)(2,1)} %bitcast.9, s32[9]{0:T(128)} %doc_hbm.1, f32[1,64]{1,0:T(1,128)} %bitcast.10, f32[1,64]{1,0:T(1,128)} %bitcast.11), custom_call_target="tpu_custom_call" | custom-call | tf_op jit(solution)/shard_map/pallas_call | solution.py:368
  110.0 0.8 copy.8

commit v5 on v4

--- a/solution.py
+++ b/solution.py
@@ -298,7 +298,7 @@
         large = scores_of(second, g, probs_b)
         outputs_of(first, g, probs_a, small)
         outputs_of(second, g, probs_b, large)
-        for c in range(2):
+        for c in (1, 0):
             for x in range(4):
                 send_home(first, g, 0, c, x)
                 send_home(second, g, 0, c, x)

time: 111 us -> 110 us (level)
  no operation moved by 1% of the time
where the time goes in v5:
time: 110 us
  Pallas kernels  109 us (99%)
    pallas_call x1, Pallas kernels, attention(): pl.pallas_call(kernel, out_shape=pltpu.VMEM((TOK, WIDTH, HEADS), bf16), i...  109 us

profile of v5, /device:TPU:1, one launch (start us, length us, event | category | flops | bytes accessed | tf_op | source)
XLA Modules:
  0.0 110.1 jit_solution(2308929572700778577)
XLA Ops:
  0.0 109.3 %shard_map.64 = bf16[32,64,128]{2,1,0:T(8,128)(2,1)S(1)} custom-call(bf16[32,64,128]{2,1,0:T(8,128)(2,1)} %bitcast.7, bf16[32,64,128]{2,1,0:T(8,128)(2,1)} %bitcast.8, bf16[32,64,128]{2,1,0:T(8,128)(2,1)} %bitcast.9, s32[9]{0:T(128)} %doc_hbm.1, f32[1,64]{1,0:T(1,128)} %bitcast.10, f32[1,64]{1,0:T(1,128)} %bitcast.11), custom_call_target="tpu_custom_call" | custom-call | tf_op jit(solution)/shard_map/pallas_call | solution.py:368
  109.3 0.8 copy.8
